TPU v7x, 32 devices: a whole 2x2x4 slice. The times are simulated.
32 devices in a mesh: dp: 4 (over z), win: 2 (over y), mp: 4 (over x, core).
Axes of the slice: x: 2, y: 2, z: 4, core: 2. Of those that a mesh axis runs over, the one named last changes fastest.
Arguments:
- tokens: bfloat16 [9408, 768], P(('dp', 'win', 'mp')), may hold values from -6 to 6
- target: bfloat16 [9408, 768], P(('dp', 'win', 'mp')), may hold values from -16 to 16
- regions: int32 [192, 49], P(('dp', 'win')), may hold values from 0 to 3
- rel_index: int32 [49, 49], replicated, may hold values from 0 to 168
- layer_norm_gain: float32 [768], replicated, may hold values from 0.5 to 1.5
- bias_table: float32 [169, 24], P(None, 'mp'), may hold values from -5 to 330
- w_qkv: bfloat16 [3, 768, 768], P(None, 'mp'), may hold values from -0.21875 to 0.21875
- w_proj: bfloat16 [768, 768], P('mp'), may hold values from -0.21875 to 0.21875
Outputs:
- input_gradient: float32 [9408, 768], P(('dp', 'win', 'mp'))
- grad_qkv: float32 [3, 768, 768], P(None, 'mp', ('dp', 'win'))
- grad_proj: float32 [768, 768], P('mp', ('dp', 'win'))
- grad_table: float32 [169, 24], P(None, 'mp')
- gain_gradient: float32 [768], replicated
- loss: float32 [], replicated
All inputs are finite; a program needn't handle non-finite values.
Results may differ from a plain program's by a relative error of at most 0.01.
Values may be sent and summed in bfloat16 or wider, within the bound.
A program may use at most 64 MiB of HBM per device.

v0:
```python
import functools

import jax
import jax.numpy as jnp
from jax import lax
from jax.experimental import pallas as pl
from jax.experimental.pallas import tpu as pltpu
from jax.sharding import PartitionSpec as P

HD = 32
WIN_TOK = 49
TABLE = 169
PAD = 64
LANES = 128
PACK = LANES // HD
MESH = pl.DeviceIdType.MESH
f32 = jnp.float32
bf16 = jnp.bfloat16
VM = pl.BlockSpec(memory_space=pltpu.VMEM)
NEG = -1e30


def greet(n_mp, n_win, n_dp):
    mp, win, dp = lax.axis_index("mp"), lax.axis_index("win"), lax.axis_index("dp")
    sem = pltpu.get_barrier_semaphore()
    peers = [{"mp": mp + 1 - 2 * lax.rem(mp, 2)}]
    peers += [{"mp": lax.rem(mp + 2 * d, n_mp)} for d in range(1, n_mp // 2)]
    peers += [{"win": lax.rem(win + d, n_win)} for d in range(1, n_win)]
    peers += [{"dp": lax.rem(dp + d, n_dp)} for d in range(1, n_dp)]
    for peer in peers:
        pl.semaphore_signal(sem, inc=1, device_id=peer, device_id_type=MESH)
    pl.semaphore_wait(sem, len(peers))


def sharing(hc, n_win):
    return max(n for n in range(1, n_win + 1) if n_win % n == 0 and hc % (16 * n) == 0)


def gather_kernel(n_mp, n_win, n_dp, wqkv, wproj, table, out, tab, send, recv, lsem):
    mp, win = lax.axis_index("mp"), lax.axis_index("win")
    hc = wproj.shape[0]
    share = sharing(hc, n_win)
    part = hc // share
    mine = lax.rem(win, share)
    n_x = n_mp // 2
    partner = mp + 1 - 2 * lax.rem(mp, 2)
    greet(n_mp, n_win, n_dp)

    def block(group):
        return out.at[:, pl.ds(pl.multiple_of(group * hc, 16), hc), :]

    def piece(group, p):
        return out.at[:, pl.ds(pl.multiple_of(group * hc + p * part, 16), part), :]

    own = [
        pltpu.make_async_copy(wqkv, out.at[pl.ds(0, 3), pl.ds(pl.multiple_of(mp * hc, 16), hc), :], lsem.at[0]),
        pltpu.make_async_copy(wproj, out.at[3, pl.ds(pl.multiple_of(mp * hc, 16), hc), :], lsem.at[1]),
        pltpu.make_async_copy(table, tab.at[mp], lsem.at[2]),
    ]
    for c in own:
        c.start()
    for c in own:
        c.wait()
    started = []
    count = [0]

    def start(src, dst, peer):
        c = pltpu.make_async_remote_copy(
            src_ref=src, dst_ref=dst, send_sem=send.at[count[0]], recv_sem=recv.at[count[0]],
            device_id=peer, device_id_type=MESH,
        )
        count[0] += 1
        c.start()
        started.append(c)
        return c

    across, tabs = [], []
    for d in range(1, n_x):
        peer = {"mp": lax.rem(mp + 2 * d, n_mp)}
        tabs.append(start(tab.at[mp], tab.at[mp], peer))
        across.append(start(piece(mp, mine), piece(mp, mine), peer))
    beside = [start(block(mp), block(mp), {"mp": partner}),
              start(tab.at[mp], tab.at[mp], {"mp": partner})]
    later = []
    for d in range(1, n_x):
        group = lax.rem(mp - 2 * d + n_mp, n_mp)
        tabs[d - 1].wait_recv()
        across[d - 1].wait_recv()
        here = []
        for e in range(1, share):
            other = win - mine + lax.rem(mine + e, share)
            here.append(start(piece(group, mine), piece(group, mine), {"win": other}))
        beside.append(start(piece(group, mine), piece(group, mine), {"mp": partner}))
        beside.append(start(tab.at[group], tab.at[group], {"mp": partner}))
        later.append((group, here))
    for group, here in later:
        for e in range(1, share):
            here[e - 1].wait_recv()
            p = lax.rem(mine - e + share, share)
            beside.append(start(piece(group, p), piece(group, p), {"mp": partner}))
    for c in beside:
        c.wait_recv()
    for c in started:
        c.wait_send()


def dot(a, b, ca, cb):
    return lax.dot_general(a, b, (((ca,), (cb,)), ((), ())), preferred_element_type=f32)


def layer_kernel(n_mp, x_ref, t_ref, gain_ref, w_ref, bias_ref, mask_ref,
                 ig_ref, g_ref, ds_ref, gg_ref, loss_ref,
                 xhat, inv, xn, qs, ks, vs, probs, at, gb, da, dq, dk, dv, dxn):
    R, C = x_ref.shape
    W = R // PAD
    ng = C // LANES
    scale = HD ** (-0.5)
    gain = gain_ref[...]
    lane_head = lax.broadcasted_iota(jnp.int32, (PAD, LANES), 1) // HD

    def rows_of(w):
        return pl.ds(pl.multiple_of(w * PAD, PAD), PAD)

    @pl.loop(0, W)
    def _(w):
        r = rows_of(w)
        xf = x_ref[r, :].astype(f32)
        cen = xf - jnp.mean(xf, axis=1, keepdims=True)
        iv = lax.rsqrt(jnp.mean(cen * cen, axis=1, keepdims=True) + 1e-05)
        xh = cen * iv
        xhat[r, :] = xh
        inv[r, :] = jnp.broadcast_to(iv, (PAD, LANES))
        xn[r, :] = (xh * gain).astype(bf16)

    BN = 256
    for t, (dst, sc) in enumerate(((qs, scale), (ks, None), (vs, None))):
        @pl.loop(0, C // BN)
        def _(j, t=t, dst=dst, sc=sc):
            c = pl.ds(pl.multiple_of(j * BN, BN), BN)
            y = dot(xn[...], w_ref[t, c, :], 1, 1)
            if sc is not None:
                y = y * sc
            dst[:, c] = y.astype(bf16)

    def spread(a):
        zero = jnp.zeros_like(a)
        return jnp.concatenate([jnp.where(lane_head == h, a, zero) for h in range(PACK)], axis=0)

    def fold(a):
        total = jnp.zeros((PAD, LANES), f32)
        for h in range(PACK):
            total = jnp.where(lane_head == h, a[h * PAD:(h + 1) * PAD], total)
        return total

    @pl.loop(0, ng)
    def _(g):
        c = pl.ds(pl.multiple_of(g * LANES, LANES), LANES)
        for w in range(W):
            r = pl.ds(w * PAD, PAD)
            s = dot(spread(ks[r, c]), qs[r, c], 1, 1)
            s = s.reshape(PACK, PAD, PAD) + bias_ref[g] + mask_ref[w][None]
            e = jnp.exp(s - jnp.max(s, axis=1, keepdims=True))
            p = e / jnp.sum(e, axis=1, keepdims=True)
            p = p.reshape(PACK * PAD, PAD)
            probs[g * W + w] = p
            at[r, c] = dot(p.astype(bf16), spread(vs[r, c]), 0, 0).astype(bf16)

    loss_ref[...] = jnp.zeros_like(loss_ref)
    @pl.loop(0, C // BN)
    def _(j):
        c = pl.ds(pl.multiple_of(j * BN, BN), BN)
        y = dot(at[...], w_ref[3, :, c], 1, 0)
        e = x_ref[:, c].astype(f32) + y - t_ref[:, c].astype(f32)
        row = lax.broadcasted_iota(jnp.int32, e.shape, 0) % PAD
        e = jnp.where(row < WIN_TOK, e, 0.0)
        ig_ref[:, c] = e
        gb[:, c] = e.astype(bf16)
        loss_ref[...] += jnp.sum(e * e, axis=0, keepdims=True)

    @pl.loop(0, C // BN)
    def _(j):
        c = pl.ds(pl.multiple_of(j * BN, BN), BN)
        da[:, c] = dot(gb[...], w_ref[3, c, :], 1, 1).astype(bf16)

    @pl.loop(0, ng)
    def _(g):
        c = pl.ds(pl.multiple_of(g * LANES, LANES), LANES)
        total = jnp.zeros((PACK * PAD, PAD), f32)
        for w in range(W):
            r = pl.ds(w * PAD, PAD)
            p = probs[g * W + w]
            do = da[r, c]
            dp = dot(spread(vs[r, c]), do, 1, 1)
            pd = (p * dp).reshape(PACK, PAD, PAD)
            ds = p.reshape(PACK, PAD, PAD) * (
                dp.reshape(PACK, PAD, PAD) - jnp.sum(pd, axis=1, keepdims=True))
            ds = ds.reshape(PACK * PAD, PAD)
            total = total + ds
            db = ds.astype(bf16)
            dv[r, c] = fold(dot(p.astype(bf16), do, 1, 0)).astype(bf16)
            dk[r, c] = fold(dot(db, qs[r, c], 1, 0)).astype(bf16)
            dq[r, c] = (dot(db, spread(ks[r, c]), 0, 0) * scale).astype(bf16)
        ds_ref[g] = total

    @pl.loop(0, C // BN)
    def _(j):
        c = pl.ds(pl.multiple_of(j * BN, BN), BN)
        y = dot(dq[...], w_ref[0, :, c], 1, 0)
        y += dot(dk[...], w_ref[1, :, c], 1, 0)
        y += dot(dv[...], w_ref[2, :, c], 1, 0)
        dxn[:, c] = y

    gg_ref[...] = jnp.zeros_like(gg_ref)

    @pl.loop(0, W)
    def _(w):
        r = rows_of(w)
        d, xh = dxn[r, :], xhat[r, :]
        gg_ref[...] += jnp.sum(d * xh, axis=0, keepdims=True)
        dh = d * gain
        m1 = jnp.mean(dh, axis=1, keepdims=True)
        m2 = jnp.mean(dh * xh, axis=1, keepdims=True)
        ig_ref[r, :] += inv[r, 0:1] * (dh - m1 - xh * m2)

    hc = C // n_mp
    xnt = xn[...].T
    gbt = gb[...].T
    for m in range(n_mp):
        lo = m * hc
        d = jnp.concatenate([a[:, lo:lo + hc] for a in (dq, dk, dv)], axis=1)
        g_ref[m] = jnp.concatenate(
            [dot(xnt, d, 1, 0).astype(bf16), dot(gbt, at[:, lo:lo + hc], 1, 0).astype(bf16)], axis=1)


def reduce_kernel(n_mp, n_win, n_dp, g_ref, small_ref, out_ref, tot_ref,
                  r_core, h, ra, rb, a1, b1, ra2, rb2, a2, rz, s_core, s1, sx, s2, sw, s3, sz,
                  send, recv):
    n_x = n_mp // 2
    mp, win, dp = lax.axis_index("mp"), lax.axis_index("win"), lax.axis_index("dp")
    core, x = lax.rem(mp, 2), mp // 2
    half = n_dp // 2
    greet(n_mp, n_win, n_dp)
    started = []

    def start(src, dst, peer):
        i = len(started)
        c = pltpu.make_async_remote_copy(
            src_ref=src, dst_ref=dst, send_sem=send.at[i], recv_sem=recv.at[i],
            device_id=peer, device_id_type=MESH,
        )
        c.start()
        started.append(c)
        return c

    def add(*terms):
        total = terms[0].astype(f32)
        for t in terms[1:]:
            total = total + t.astype(f32)
        return total

    def on_x(d):
        return {"mp": lax.rem(mp + 2 * d, n_mp)}, lax.rem(x + d, n_x)

    def on_win(d):
        return {"win": lax.rem(win + d, n_win)}, lax.rem(win + d, n_win)

    def on_dp(d):
        return {"dp": lax.rem(dp + d, n_dp)}, lax.rem(dp + d, n_dp)

    partner = {"mp": mp + 1 - 2 * core}
    c0 = start(small_ref, s_core, partner)
    firsts = [start(g_ref.at[i, 1 - core], r_core.at[i], partner) for i in range(n_x)]
    c0.wait_recv()
    s1[...] = small_ref[...] + s_core[...]

    def exchange_small(src, slots, on, n, own):
        cs = [start(src, slots.at[own], on(d)[0]) for d in range(1, n)]
        return cs

    def finish_small(cs, src, slots, own, n, dst):
        slots[own] = src[...]
        for c in cs:
            c.wait_recv()
        total = slots[0]
        for i in range(1, n):
            total = total + slots[i]
        dst[...] = total

    cx = exchange_small(s1, sx, on_x, n_x, x)
    for i in range(n_x):
        firsts[i].wait_recv()
        h[i] = add(g_ref[i, core], r_core[i]).astype(bf16)
    ca = [start(h.at[on_x(d)[1], :, pl.ds(0, half)], ra.at[d - 1], on_x(d)[0]) for d in range(1, n_x)]
    cb = [start(h.at[:, on_win(d)[1], pl.ds(half, half)], rb.at[d - 1], on_win(d)[0])
          for d in range(1, n_win)]
    finish_small(cx, s1, sx, x, n_x, s2)
    cw = exchange_small(s2, sw, on_win, n_win, win)
    for c in ca:
        c.wait_recv()
    a1[...] = add(h[x, :, 0:half], *[ra[d] for d in range(n_x - 1)]).astype(bf16)
    ca = [start(a1.at[on_win(d)[1]], ra2.at[d - 1], on_win(d)[0]) for d in range(1, n_win)]
    for c in cb:
        c.wait_recv()
    b1[...] = add(h[:, win, half:2 * half], *[rb[d] for d in range(n_win - 1)]).astype(bf16)
    cb = [start(b1.at[on_x(d)[1]], rb2.at[d - 1], on_x(d)[0]) for d in range(1, n_x)]
    finish_small(cw, s2, sw, win, n_win, s3)
    cz = exchange_small(s3, sz, on_dp, n_dp, dp)
    for c in ca:
        c.wait_recv()
    a2[0:half] = add(a1[win], *[ra2[d] for d in range(n_win - 1)]).astype(bf16)
    for c in cb:
        c.wait_recv()
    a2[half:2 * half] = add(b1[x], *[rb2[d] for d in range(n_x - 1)]).astype(bf16)
    zs = [start(a2.at[on_dp(d)[1]], rz.at[d - 1], on_dp(d)[0]) for d in range(1, n_dp)]
    finish_small(cz, s3, sz, dp, n_dp, tot_ref)
    for c in zs:
        c.wait_recv()
    out_ref[...] = add(a2[dp], *[rz[d] for d in range(n_dp - 1)])
    for c in started:
        c.wait_send()


def per_device(sizes, tokens, target, regions, rel_index, gain, bias_table, w_qkv, w_proj):
    n_dp, n_win, n_mp = sizes
    n_x = n_mp // 2
    rows, C = tokens.shape
    W = rows // WIN_TOK
    hc = w_proj.shape[0]
    nh = hc // HD
    heads = nh * n_mp
    R = W * PAD
    ng = C // LANES
    everyone = rows * n_dp * n_win * n_mp
    SDS = jax.ShapeDtypeStruct
    big = 60 * 1024 * 1024

    copies = 2 * (n_x - 1) + 2 + (n_x - 1) * (2 * (sharing(hc, n_win) - 1) + 2)
    table = jnp.pad(bias_table.T, ((0, 8 - nh), (0, 2 * LANES - TABLE)))
    weights, tables = pl.pallas_call(
        functools.partial(gather_kernel, n_mp, n_win, n_dp),
        out_shape=(SDS((4, C, C), bf16), SDS((n_mp, 8, 2 * LANES), f32)),
        in_specs=[VM] * 3, out_specs=(VM, VM),
        scratch_shapes=[pltpu.SemaphoreType.DMA((copies,)), pltpu.SemaphoreType.DMA((copies,)),
                        pltpu.SemaphoreType.DMA((3,))],
        compiler_params=pltpu.CompilerParams(collective_id=0, has_side_effects=True),
        name="gather",
    )(w_qkv, w_proj, table)

    index = jnp.pad(rel_index.T, ((0, PAD - WIN_TOK), (0, PAD - WIN_TOK)), constant_values=-1)
    onehot = (index.reshape(-1)[None, :] == jnp.arange(2 * LANES, dtype=jnp.int32)[:, None]).astype(f32)
    full = tables[:, :nh].reshape(heads, 2 * LANES)
    bias = jnp.dot(full, onehot, precision=lax.Precision.HIGHEST).reshape(ng, PACK, PAD, PAD)
    key_pad = jnp.where(jnp.arange(PAD) < WIN_TOK, 0.0, NEG)[:, None]
    bias = bias + key_pad
    mine = lax.dynamic_slice_in_dim(regions, lax.axis_index("mp") * W, W, 0)
    mine = jnp.pad(mine, ((0, 0), (0, PAD - WIN_TOK)))
    maskv = jnp.where(mine[:, :, None] == mine[:, None, :], 0.0, -100.0).astype(f32)

    def padded(a):
        a = a.reshape(W, WIN_TOK, C)
        return jnp.pad(a, ((0, 0), (0, PAD - WIN_TOK), (0, 0))).reshape(R, C)

    act = pltpu.VMEM((R, C), bf16)
    wide = pltpu.VMEM((R, C), f32)
    ig, grads, ds, gg, loss = pl.pallas_call(
        functools.partial(layer_kernel, n_mp),
        out_shape=(SDS((R, C), f32), SDS((n_mp, C, 4 * hc), bf16), SDS((ng, PACK * PAD, PAD), f32),
                   SDS((1, C), f32), SDS((1, 256), f32)),
        in_specs=[VM] * 6, out_specs=(VM,) * 5,
        scratch_shapes=[wide, pltpu.VMEM((R, LANES), f32), act, act, act, act,
                        pltpu.VMEM((ng * W, PACK * PAD, PAD), f32),
                        act, act, act, act, act, act, wide],
        compiler_params=pltpu.CompilerParams(vmem_limit_bytes=big),
        name="layer",
    )(padded(tokens), padded(target), gain[None, :], weights, bias, maskv)

    dtab = jnp.dot(ds.reshape(heads, PAD * PAD), onehot.T, precision=lax.Precision.HIGHEST)
    extra = jnp.concatenate([gg.reshape(C // 256, 256), loss], axis=0)
    small = jnp.concatenate([dtab, extra], axis=0)
    small = jnp.pad(small, ((0, -small.shape[0] % 8), (0, 0)))
    cpd = C // (n_dp * n_win)
    L = 4 * hc
    half = n_dp // 2
    grads = grads.reshape(n_x, 2, n_dp, n_win, cpd, L).transpose(0, 1, 3, 2, 4, 5)
    sm = small.shape
    copies = 1 + n_x + 3 * (n_x - 1) + 3 * (n_win - 1) + 2 * (n_dp - 1)
    V = pltpu.VMEM
    out, tot = pl.pallas_call(
        functools.partial(reduce_kernel, n_mp, n_win, n_dp),
        out_shape=(SDS((cpd, L), f32), SDS(sm, f32)),
        in_specs=[VM] * 2, out_specs=(VM, VM),
        scratch_shapes=[
            V((n_x, n_win, n_dp, cpd, L), bf16),
            V((n_x, n_win, n_dp, cpd, L), bf16),
            V((max(n_x - 1, 1), n_win, half, cpd, L), bf16),
            V((max(n_win - 1, 1), n_x, half, cpd, L), bf16),
            V((n_win, half, cpd, L), bf16),
            V((n_x, half, cpd, L), bf16),
            V((max(n_win - 1, 1), half, cpd, L), bf16),
            V((max(n_x - 1, 1), half, cpd, L), bf16),
            V((n_dp, cpd, L), bf16),
            V((n_dp - 1, cpd, L), bf16),
            V(sm, f32), V(sm, f32), V((n_x,) + sm, f32), V(sm, f32), V((n_win,) + sm, f32),
            V(sm, f32), V((n_dp,) + sm, f32),
            pltpu.SemaphoreType.DMA((copies,)), pltpu.SemaphoreType.DMA((copies,)),
        ],
        compiler_params=pltpu.CompilerParams(
            collective_id=1, has_side_effects=True, vmem_limit_bytes=big),
        name="reduce",
    )(grads, small)

    s = everyone ** (-0.5)
    out = (out * s).reshape(cpd, 4, hc).transpose(1, 2, 0)
    tot_heads = lax.dynamic_slice_in_dim(tot[:heads, :TABLE], lax.axis_index("mp") * nh, nh, 0)
    gain_gradient = tot[heads:heads + C // 256].reshape(C) * s
    loss = 0.5 * jnp.sum(tot[heads + C // 256]) / everyone
    return (ig.reshape(W, PAD, C)[:, :WIN_TOK].reshape(rows, C), out[:3], out[3],
            tot_heads.T * s, gain_gradient, loss)


def solution(mesh):
    sizes = (mesh.shape["dp"], mesh.shape["win"], mesh.shape["mp"])
    in_specs = (
        P(("dp", "win", "mp"), None),
        P(("dp", "win", "mp"), None),
        P(("dp", "win"), None),
        P(),
        P(),
        P(None, "mp"),
        P(None, "mp", None),
        P("mp", None),
    )
    out_specs = (
        P(("dp", "win", "mp"), None),
        P(None, "mp", ("dp", "win")),
        P("mp", ("dp", "win")),
        P(None, "mp"),
        P(),
        P(),
    )
    return jax.shard_map(
        functools.partial(per_device, sizes), mesh=mesh, in_specs=in_specs, out_specs=out_specs,
        check_vma=False,
    )
```

profile of v0, /device:TPU:0, one launch (start us, length us, event | category | flops | bytes accessed | tf_op | source)
XLA Modules:
  0.0 153.2 jit_solution(11293233775287131423)
XLA Ops:
  0.6 0.0 copy-start
  0.7 1.3 broadcast_in_dim.22.gain_ref
  2.0 1.3 pad.25.table
  3.3 0.8 copy.30
  4.1 0.1 eq.54
  4.2 0.8 compare_select_fusion.mask_ref
  5.0 1.2 reshape.73
  6.1 0.9 pad.23
  7.0 1.2 reshape.75
  8.2 0.9 pad.24
  9.0 39.1 %gather.1 = (bf16[4,768,768]{2,1,0:T(8,128)(2,1)}, f32[4,8,256]{2,1,0:T(8,128)}) custom-call(bf16[3,192,768]{2,1,0:T(8,128)(2,1)} %wqkv.1, bf16[192,768]{1,0:T(8,128)(2,1)} %wproj.1, f32[8,256]{1,0:T(8,128)} %pad.25.table), custom_call_target="tpu_custom_call" | custom-call | tf_op jit(solution)/shard_map/gather/pallas_call | solution.py:339
  48.1 0.8 dot_general.8
  48.9 2.9 %fusion.1 = f32[6,4,64,64]{3,1,2,0:T(4,128)S(1)} fusion(s32[64,64]{1,0:T(8,128)S(1)} %pad.26.clone, f32[6,4,256]{2,1,0:T(4,128)S(1)} %dot_general.8), kind=kOutput, calls=%fused_computation.4 | convolution fusion | flops 303038464 | bytes 434176 | tf_op jit(solution)/shard_map/dot_general | solution.py:352
  51.8 1.0 copy_add_fusion.bias_ref
  52.8 37.1 %layer.1 = (f32[384,768]{1,0:T(8,128)}, bf16[4,768,768]{2,1,0:T(8,128)(2,1)}, f32[6,256,64]{2,1,0:T(8,128)}, f32[1,768]{1,0:T(1,128)}, f32[1,256]{1,0:T(1,128)}) custom-call(bf16[384,768]{1,0:T(8,128)(2,1)} %bitcast.29, bf16[384,768]{1,0:T(8,128)(2,1)} %bitcast.30, f32[1,768]{1,0:T(1,128)} %broadcast_in_dim.22.gain_ref, ...), custom_call_target="tpu_custom_call" | custom-call | tf_op jit(solution)/shard_map/layer/pallas_call | solution.py:365
  89.9 1.3 slice.28
  91.2 1.1 reshape.78
  92.3 4.9 %copy.33 = bf16[2,2,4,2,96,768]{5,4,2,3,1,0:T(8,128)(2,1)} copy(bf16[2,2,4,2,96,768]{5,4,3,2,1,0:T(8,128)(2,1)} %bitcast.28) | data formatting | bytes 9437184 | tf_op jit(solution)/shard_map/reshape | solution.py:384
  97.2 0.0 copy-done.2
  97.2 0.3 reshape.80
  97.5 2.0 %fusion.3 = f32[24,256]{1,0:T(8,128)S(1)} fusion(f32[24,4096]{1,0:T(8,128)S(1)} %reshape.80, s32[4096]{0:T(1024)S(1)} %eq.54), kind=kOutput, calls=%fused_computation.5 | convolution fusion | flops 303038464 | bytes 434176 | tf_op jit(solution)/shard_map/dot_general | solution.py:377
  99.5 0.6 select_maximum_fusion.small_ref
  100.1 44.8 %reduce.3 = (f32[96,768]{1,0:T(8,128)}, f32[32,256]{1,0:T(8,128)}) custom-call(bf16[2,2,2,4,96,768]{5,4,3,2,1,0:T(8,128)(2,1)} %bitcast.27, f32[32,256]{1,0:T(8,128)} %select_maximum_fusion.small_ref), custom_call_target="tpu_custom_call" | custom-call | tf_op jit(solution)/shard_map/reduce/pallas_call | solution.py:388
  144.9 1.3 slice_reduce_fusion
  146.9 1.0 broadcast_multiply_fusion
  147.8 0.7 slice_multiply_fusion
  148.5 0.7 slice.25
  149.3 0.6 multiply_bitcast_fusion
  149.9 0.6 mul.36
  150.5 0.2 copy.29
  150.7 0.7 slice_bitcast_fusion
  151.3 0.7 slice.29
  (12 shorter events, 0.1 us)
Async XLA Ops:
  0.6 1.3 copy-start
  92.3 4.9 %copy-start.2 = (f32[1,768]{1,0:T(1,128)S(1)}, f32[1,768]{1,0:T(1,128)}, u32[]{:S(2)}) copy-start(f32[1,768]{1,0:T(1,128)} %get-tuple-element.20) | copy-start | bytes 9220
  92.3 4.9 %copy-start.1 = (f32[6,256,64]{2,1,0:T(8,128)S(1)}, f32[6,256,64]{2,1,0:T(8,128)}, u32[]{:S(2)}) copy-start(f32[6,256,64]{2,1,0:T(8,128)} %get-tuple-element.19) | copy-start | bytes 1179652
  92.3 7.2 %copy-start.3 = (f32[1,256]{1,0:T(1,128)S(1)}, f32[1,256]{1,0:T(1,128)}, u32[]{:S(2)}) copy-start(f32[1,256]{1,0:T(1,128)} %get-tuple-element.21) | copy-start | bytes 3076
where the time goes:
time: 154 us; the launch traced here: 153 us
  Pallas kernels  121 us (79%)
  local copies, waits for them, and re-layouts  18.8 us (12%)
  other arithmetic  6.08 us (4%)
  matrix products  4.84 us (3%)
  between operations  2.51 us (2%)
    pallas_call x1, Pallas kernels, per_device(): pl.pallas_call(functools.partial(reduce_kernel, n_mp, n_win, n_dp), out_s...  44.8 us
    pallas_call x1, Pallas kernels, per_device(): pl.pallas_call(functools.partial(gather_kernel, n_mp, n_win, n_dp), out_s...  39.1 us
    pallas_call x1, Pallas kernels, per_device(): pl.pallas_call(functools.partial(layer_kernel, n_mp), out_shape=(SDS((R,...  37.1 us
    reshape x1, local copies, waits for them, and re-layouts, per_device(): grads.reshape(n_x, 2, n_dp, n_win, cpd, L).transpose(0, 1, 3, 2, 4, 5)  4.89 us

commit v1 on v0

v1 whole, which is shorter than its diff:
```python
import functools

import jax
import jax.numpy as jnp
from jax import lax
from jax.experimental import pallas as pl
from jax.experimental.pallas import tpu as pltpu
from jax.sharding import PartitionSpec as P

HD = 32
WIN_TOK = 49
TABLE = 169
PAD = 64
LANES = 128
PACK = LANES // HD
MESH = pl.DeviceIdType.MESH
f32 = jnp.float32
bf16 = jnp.bfloat16
VM = pl.BlockSpec(memory_space=pltpu.VMEM)
NEG = -1e30


def greet(n_mp, n_win, n_dp):
    mp, win, dp = lax.axis_index("mp"), lax.axis_index("win"), lax.axis_index("dp")
    sem = pltpu.get_barrier_semaphore()
    peers = [{"mp": mp + 1 - 2 * lax.rem(mp, 2)}]
    peers += [{"mp": lax.rem(mp + 2 * d, n_mp)} for d in range(1, n_mp // 2)]
    peers += [{"win": lax.rem(win + d, n_win)} for d in range(1, n_win)]
    peers += [{"dp": lax.rem(dp + d, n_dp)} for d in range(1, n_dp)]
    for peer in peers:
        pl.semaphore_signal(sem, inc=1, device_id=peer, device_id_type=MESH)
    pl.semaphore_wait(sem, len(peers))


def sharing(hc, n_win):
    return max(n for n in range(1, n_win + 1) if n_win % n == 0 and hc % (16 * n) == 0)


def dot(a, b, ca, cb):
    return lax.dot_general(a, b, (((ca,), (cb,)), ((), ())), preferred_element_type=f32)


class Link:
    def __init__(self, send, recv):
        self.send, self.recv, self.started = send, recv, []

    def __call__(self, src, dst, peer):
        i = len(self.started)
        c = pltpu.make_async_remote_copy(
            src_ref=src, dst_ref=dst, send_sem=self.send.at[i], recv_sem=self.recv.at[i],
            device_id=peer, device_id_type=MESH,
        )
        c.start()
        self.started.append(c)
        return c


def add(*terms):
    total = terms[0].astype(f32)
    for t in terms[1:]:
        total = total + t.astype(f32)
    return total


def layer_kernel(n_mp, n_win, n_dp, everyone,
                 x_ref, t_ref, gain_ref, wqkv, wproj, table, index_ref, mask_ref,
                 ig_ref, out_ref, tot_ref,
                 w_ref, tab, bias, xt, xhat, inv, xn, qs, ks, vs, probs, at, gb, da, dq, dk, dv, dxn,
                 ds_ref, gg, sq, small,
                 g_ref, r_core, h, ra, rb, a1, b1, ra2, rb2, a2, rz,
                 s_core, s1, sx, s2, sw, s3, sz, send, recv, lsem):
    mp, win, dp = lax.axis_index("mp"), lax.axis_index("win"), lax.axis_index("dp")
    core, x = lax.rem(mp, 2), mp // 2
    R, C = xhat.shape
    W = R // PAD
    ng = C // LANES
    hc = C // n_mp
    nh = hc // HD
    n_x = n_mp // 2
    cpd = C // (n_dp * n_win)
    half = n_dp // 2
    share = sharing(hc, n_win)
    part = hc // share
    mine = lax.rem(win, share)
    scale = HD ** (-0.5)
    partner = {"mp": mp + 1 - 2 * core}
    start = Link(send, recv)
    BN = 256

    def across(group, size=hc, off=0):
        return pl.ds(pl.multiple_of(group * hc + off, 16), size)

    def own(t, rows):
        return wqkv.at[t, rows, :] if t < 3 else wproj.at[rows, :]

    local = [pltpu.make_async_copy(own(t, pl.ds(0, hc)), w_ref.at[t, across(mp), :], lsem.at[t])
             for t in range(4)]
    local.append(pltpu.make_async_copy(table, tab.at[mp], lsem.at[4]))
    for c in local:
        c.start()
    greet(n_mp, n_win, n_dp)
    tabx = [start(table, tab.at[mp], {"mp": lax.rem(mp + 2 * d, n_mp)}) for d in range(1, n_x)]
    tabs = [start(table, tab.at[mp], partner)]
    first, ready = [], []
    for t in range(4):
        first.append([])
        for d in range(1, n_x):
            first[t].append(start(
                own(t, pl.ds(pl.multiple_of(mine * part, 16), part)),
                w_ref.at[t, across(mp, part, mine * part), :], {"mp": lax.rem(mp + 2 * d, n_mp)}))
    for t in range(4):
        ready.append([start(own(t, pl.ds(0, hc)), w_ref.at[t, across(mp), :], partner)])

    second = [[] for _ in range(4)]

    def pass_on(t):
        for d in range(1, n_x):
            group = lax.rem(mp - 2 * d + n_mp, n_mp)
            ref = w_ref.at[t, across(group, part, mine * part), :]
            first[t][d - 1].wait_recv()
            for e in range(1, share):
                other = win - mine + lax.rem(mine + e, share)
                second[t].append((group, e, start(ref, ref, {"win": other})))
            ready[t].append(start(ref, ref, partner))

    def pass_rest(t):
        for group, e, c in second[t]:
            c.wait_recv()
            p = lax.rem(mine - e + share, share)
            ref = w_ref.at[t, across(group, part, p * part), :]
            ready[t].append(start(ref, ref, partner))

    def complete(t):
        for c in ready[t]:
            c.wait_recv()

    gain = gain_ref[...]
    lane_head = lax.broadcasted_iota(jnp.int32, (PAD, LANES), 1) // HD
    blank = jnp.zeros((PAD - WIN_TOK, C), f32)
    for w in range(W):
        r = pl.ds(w * PAD, PAD)
        src = pl.ds(w * WIN_TOK, WIN_TOK)
        xf = jnp.concatenate([x_ref[src, :].astype(f32), blank], axis=0)
        tf = jnp.concatenate([t_ref[src, :].astype(f32), blank], axis=0)
        xt[r, :] = xf - tf
        cen = xf - jnp.mean(xf, axis=1, keepdims=True)
        iv = lax.rsqrt(jnp.mean(cen * cen, axis=1, keepdims=True) + 1e-05)
        xh = cen * iv
        xhat[r, :] = xh
        inv[r, :] = jnp.broadcast_to(iv, (PAD, LANES))
        xn[r, :] = (xh * gain).astype(bf16)
    for d in range(1, n_x):
        group = lax.rem(mp - 2 * d + n_mp, n_mp)
        tabx[d - 1].wait_recv()
        tabs.append(start(tab.at[group], tab.at[group], partner))
    for c in local:
        c.wait()
    for c in tabs:
        c.wait_recv()
    pass_on(0)

    entries = lax.broadcasted_iota(jnp.int32, (2 * LANES, PAD), 0)

    def thirds(a):
        hi = a.astype(bf16)
        rest = a - hi.astype(f32)
        mid = rest.astype(bf16)
        low = (rest - mid.astype(f32)).astype(bf16)
        return jnp.concatenate([hi, mid, low], axis=0)

    tabn = 8 * n_mp
    table3 = thirds(tab[...].reshape(tabn, 2 * LANES))

    def fill_bias(lo, hi):
        @pl.loop(lo // 8, hi // 8)
        def _(kk):
            for u in range(8):
                k = kk * 8 + u
                onehot = (entries == index_ref[pl.ds(k, 1), :]).astype(f32).astype(bf16)
                b = dot(table3, onehot, 1, 0)
                b = b[:tabn] + b[tabn:2 * tabn] + b[2 * tabn:]
                b = b + jnp.where(k < WIN_TOK, 0.0, NEG)
                for head in range(n_mp * nh):
                    row = head // nh * 8 + head % nh
                    bias[head // PACK, pl.ds(head % PACK * PAD + k, 1), :] = b[row:row + 1]

    fill_bias(0, PAD // 2)
    pass_on(1)
    fill_bias(PAD // 2, PAD)

    def project(t, dst, sc):
        @pl.loop(0, C // BN)
        def _(j):
            c = pl.ds(pl.multiple_of(j * BN, BN), BN)
            y = dot(xn[...], w_ref[t, c, :], 1, 1)
            if sc is not None:
                y = y * sc
            dst[:, c] = y.astype(bf16)

    pass_rest(0)
    pass_on(2)
    complete(0)
    project(0, qs, scale)
    pass_rest(1)
    pass_on(3)
    complete(1)
    project(1, ks, None)
    pass_rest(2)
    complete(2)
    project(2, vs, None)

    def spread(a):
        zero = jnp.zeros_like(a)
        return jnp.concatenate([jnp.where(lane_head == i, a, zero) for i in range(PACK)], axis=0)

    def fold(a):
        total = jnp.zeros((PAD, LANES), f32)
        for i in range(PACK):
            total = jnp.where(lane_head == i, a[i * PAD:(i + 1) * PAD], total)
        return total

    def forward(lo, hi):
        @pl.loop(lo, hi)
        def _(g):
            c = pl.ds(pl.multiple_of(g * LANES, LANES), LANES)
            for w in range(W):
                r = pl.ds(w * PAD, PAD)
                s = dot(spread(ks[r, c]), qs[r, c], 1, 1) + bias[g]
                s = s.reshape(PACK, PAD, PAD) + mask_ref[w][None]
                e = jnp.exp(s - jnp.max(s, axis=1, keepdims=True))
                p = e / jnp.sum(e, axis=1, keepdims=True)
                p = p.reshape(PACK * PAD, PAD)
                probs[g * W + w] = p
                at[r, c] = dot(p.astype(bf16), spread(vs[r, c]), 0, 0).astype(bf16)

    forward(0, ng // 3)
    pass_rest(3)
    forward(ng // 3, ng)
    complete(3)

    sq[...] = jnp.zeros_like(sq)

    @pl.loop(0, C // BN)
    def _(j):
        c = pl.ds(pl.multiple_of(j * BN, BN), BN)
        e = xt[:, c] + dot(at[...], w_ref[3, :, c], 1, 0)
        row = lax.broadcasted_iota(jnp.int32, e.shape, 0) % PAD
        e = jnp.where(row < WIN_TOK, e, 0.0)
        xt[:, c] = e
        gb[:, c] = e.astype(bf16)
        sq[...] += jnp.sum(e * e, axis=0, keepdims=True)

    @pl.loop(0, C // BN)
    def _(j):
        c = pl.ds(pl.multiple_of(j * BN, BN), BN)
        da[:, c] = dot(gb[...], w_ref[3, c, :], 1, 1).astype(bf16)

    @pl.loop(0, ng)
    def _(g):
        c = pl.ds(pl.multiple_of(g * LANES, LANES), LANES)
        total = jnp.zeros((PACK * PAD, PAD), f32)
        for w in range(W):
            r = pl.ds(w * PAD, PAD)
            p = probs[g * W + w]
            do = da[r, c]
            dprob = dot(spread(vs[r, c]), do, 1, 1)
            p3, d3 = p.reshape(PACK, PAD, PAD), dprob.reshape(PACK, PAD, PAD)
            ds = p3 * (d3 - jnp.sum(p3 * d3, axis=1, keepdims=True))
            ds = ds.reshape(PACK * PAD, PAD)
            total = total + ds
            db = ds.astype(bf16)
            dv[r, c] = fold(dot(p.astype(bf16), do, 1, 0)).astype(bf16)
            dk[r, c] = fold(dot(db, qs[r, c], 1, 0)).astype(bf16)
            dq[r, c] = (dot(db, spread(ks[r, c]), 0, 0) * scale).astype(bf16)
        ds_ref[g] = total

    waves = 2 if cpd % 32 == 0 else 1
    deep = cpd // waves
    xnt = xn[...].T
    gbt = gb[...].T
    firsts = []
    for i in range(n_x):
        for cc in range(2):
            lo = (2 * i + cc) * hc
            d = jnp.concatenate([a[:, lo:lo + hc] for a in (dq, dk, dv)], axis=1)
            y = jnp.concatenate(
                [dot(xnt, d, 1, 0), dot(gbt, at[:, lo:lo + hc], 1, 0)], axis=1)
            for u in range(n_dp):
                for v in range(n_win):
                    o = (u * n_win + v) * cpd
                    g_ref[i, cc, v, u] = y[o:o + cpd].astype(bf16)
        firsts.append([start(g_ref.at[i, 1 - core, :, :, pl.ds(f * deep, deep)],
                             r_core.at[i, :, :, pl.ds(f * deep, deep)], partner)
                       for f in range(waves)])

    def on_x(d):
        return {"mp": lax.rem(mp + 2 * d, n_mp)}, lax.rem(x + d, n_x)

    def on_win(d):
        return {"win": lax.rem(win + d, n_win)}, lax.rem(win + d, n_win)

    def on_dp(d):
        return {"dp": lax.rem(dp + d, n_dp)}, lax.rem(dp + d, n_dp)

    def rows(f):
        return pl.ds(f * deep, deep)

    lo_dp, hi_dp = pl.ds(0, half), pl.ds(half, half)
    stage = {}

    def step1(f):
        for i in range(n_x):
            firsts[i][f].wait_recv()
            h[i, :, :, rows(f)] = add(g_ref[i, core, :, :, rows(f)],
                                      r_core[i, :, :, rows(f)]).astype(bf16)
        ca = [start(h.at[on_x(d)[1], :, lo_dp, rows(f)], ra.at[d - 1, :, :, rows(f)], on_x(d)[0])
              for d in range(1, n_x)]
        cb = [start(h.at[:, on_win(d)[1], hi_dp, rows(f)], rb.at[d - 1, :, :, rows(f)], on_win(d)[0])
              for d in range(1, n_win)]
        stage[f] = ca, cb

    def step2(f):
        ca, cb = stage[f]
        for c in ca:
            c.wait_recv()
        a1[:, :, rows(f)] = add(h[x, :, lo_dp, rows(f)],
                                *[ra[d, :, :, rows(f)] for d in range(n_x - 1)]).astype(bf16)
        na = [start(a1.at[on_win(d)[1], :, rows(f)], ra2.at[d - 1, :, rows(f)], on_win(d)[0])
              for d in range(1, n_win)]
        for c in cb:
            c.wait_recv()
        b1[:, :, rows(f)] = add(h[:, win, hi_dp, rows(f)],
                                *[rb[d, :, :, rows(f)] for d in range(n_win - 1)]).astype(bf16)
        nb = [start(b1.at[on_x(d)[1], :, rows(f)], rb2.at[d - 1, :, rows(f)], on_x(d)[0])
              for d in range(1, n_x)]
        stage[f] = na, nb

    def step3(f):
        ca, cb = stage[f]
        for c in ca:
            c.wait_recv()
        a2[lo_dp, rows(f)] = add(a1[win, :, rows(f)],
                                 *[ra2[d, :, rows(f)] for d in range(n_win - 1)]).astype(bf16)
        for c in cb:
            c.wait_recv()
        a2[hi_dp, rows(f)] = add(b1[x, :, rows(f)],
                                 *[rb2[d, :, rows(f)] for d in range(n_x - 1)]).astype(bf16)
        stage[f] = [start(a2.at[on_dp(d)[1], rows(f)], rz.at[d - 1, rows(f)], on_dp(d)[0])
                    for d in range(1, n_dp)]

    def step4(f):
        for c in stage[f]:
            c.wait_recv()
        y = add(a2[dp, rows(f)], *[rz[d, rows(f)] for d in range(n_dp - 1)])
        out_ref[rows(f), :] = y * everyone ** (-0.5)

    for f in range(waves):
        step1(f)

    @pl.loop(0, C // BN)
    def _(j):
        c = pl.ds(pl.multiple_of(j * BN, BN), BN)
        y = dot(dq[...], w_ref[0, :, c], 1, 0)
        y += dot(dk[...], w_ref[1, :, c], 1, 0)
        y += dot(dv[...], w_ref[2, :, c], 1, 0)
        dxn[:, c] = y

    gg[...] = jnp.zeros_like(gg)

    def finish(w):
        r = pl.ds(w * PAD, PAD)
        d, xh = dxn[r, :], xhat[r, :]
        gg[...] += jnp.sum(d * xh, axis=0, keepdims=True)
        dh = d * gain
        m1 = jnp.mean(dh, axis=1, keepdims=True)
        m2 = jnp.mean(dh * xh, axis=1, keepdims=True)
        y = xt[r, :] + inv[r, 0:1] * (dh - m1 - xh * m2)
        ig_ref[pl.ds(w * WIN_TOK, WIN_TOK), :] = y[:WIN_TOK]

    for w in range(W):
        finish(w)

    step2(0)
    heads = n_mp * nh
    small[...] = jnp.zeros_like(small)
    hp = ng * PACK

    @pl.loop(0, PAD // 8)
    def _(kk):
        total = jnp.zeros((3 * hp, 2 * LANES), f32)
        for u in range(8):
            k = kk * 8 + u
            onehot = (entries == index_ref[pl.ds(k, 1), :]).astype(f32).astype(bf16)
            one = jnp.concatenate(
                [ds_ref[i // PACK, pl.ds(i % PACK * PAD + k, 1), :] for i in range(hp)], axis=0)
            total = total + dot(thirds(one), onehot, 1, 1)
        small[0:hp, :] += total[:hp] + total[hp:2 * hp] + total[2 * hp:]

    for i in range(C // BN):
        small[heads + i:heads + i + 1, :] = gg[:, i * BN:(i + 1) * BN]
    small[heads + C // BN:heads + C // BN + 1, :] = sq[...]

    cc0 = start(small, s_core, partner)
    for f in range(1, waves):
        step2(f)

    def share_small(src, slots, on, n):
        def begin(me):
            return [start(src, slots.at[me], on(d)[0]) for d in range(1, n)]
        return begin

    def finish_small(cs, src, slots, me, n, dst):
        slots[me] = src[...]
        for c in cs:
            c.wait_recv()
        total = slots[0]
        for i in range(1, n):
            total = total + slots[i]
        dst[...] = total

    cc0.wait_recv()
    s1[...] = small[...] + s_core[...]
    cx = share_small(s1, sx, on_x, n_x)(x)
    step3(0)
    finish_small(cx, s1, sx, x, n_x, s2)
    cw = share_small(s2, sw, on_win, n_win)(win)
    finish_small(cw, s2, sw, win, n_win, s3)
    cz = share_small(s3, sz, on_dp, n_dp)(dp)
    for f in range(1, waves):
        step3(f)
    finish_small(cz, s3, sz, dp, n_dp, tot_ref)
    for f in range(waves):
        step4(f)
    for c in start.started:
        c.wait_send()


def per_device(sizes, tokens, target, regions, rel_index, gain, bias_table, w_qkv, w_proj):
    n_dp, n_win, n_mp = sizes
    n_x = n_mp // 2
    rows, C = tokens.shape
    W = rows // WIN_TOK
    hc = w_proj.shape[0]
    nh = hc // HD
    heads = nh * n_mp
    R = W * PAD
    ng = C // LANES
    everyone = rows * n_dp * n_win * n_mp
    SDS = jax.ShapeDtypeStruct
    V = pltpu.VMEM

    table = jnp.pad(bias_table.T, ((0, 8 - nh), (0, 2 * LANES - TABLE)))
    index = jnp.pad(rel_index.T, ((0, PAD - WIN_TOK), (0, PAD - WIN_TOK)), constant_values=-1)
    mine = lax.dynamic_slice_in_dim(regions, lax.axis_index("mp") * W, W, 0)
    mine = jnp.pad(mine, ((0, 0), (0, PAD - WIN_TOK)))
    maskv = jnp.where(mine[:, :, None] == mine[:, None, :], 0.0, -100.0).astype(f32)

    cpd = C // (n_dp * n_win)
    L = 4 * hc
    half = n_dp // 2
    waves = 2 if cpd % 32 == 0 else 1
    share = sharing(hc, n_win)
    copies = n_x + 4 * (n_x - 1) + 4 + (n_x - 1) * (1 + 4 * (2 * (share - 1) + 1))
    copies += waves * (n_x + 2 * (n_x - 1) + 2 * (n_win - 1) + n_dp - 1)
    copies += 1 + (n_x - 1) + (n_win - 1) + (n_dp - 1)
    srows = heads + C // 256 + 1
    sm = (srows + -srows % 8, 256)
    act = V((R, C), bf16)
    wide = V((R, C), f32)
    ig, out, tot = pl.pallas_call(
        functools.partial(layer_kernel, n_mp, n_win, n_dp, everyone),
        out_shape=(SDS((rows, C), f32), SDS((cpd, L), f32), SDS(sm, f32)),
        in_specs=[VM] * 8, out_specs=(VM,) * 3,
        scratch_shapes=[
            V((4, C, C), bf16), V((n_mp, 8, 2 * LANES), f32), V((ng, PACK * PAD, PAD), f32),
            wide, wide, V((R, LANES), f32), act, act, act, act,
            V((ng * W, PACK * PAD, PAD), f32),
            act, act, act, act, act, act, wide,
            V((ng, PACK * PAD, PAD), f32), V((1, C), f32), V((1, 256), f32), V(sm, f32),
            V((n_x, 2, n_win, n_dp, cpd, L), bf16),
            V((n_x, n_win, n_dp, cpd, L), bf16),
            V((n_x, n_win, n_dp, cpd, L), bf16),
            V((max(n_x - 1, 1), n_win, half, cpd, L), bf16),
            V((max(n_win - 1, 1), n_x, half, cpd, L), bf16),
            V((n_win, half, cpd, L), bf16),
            V((n_x, half, cpd, L), bf16),
            V((max(n_win - 1, 1), half, cpd, L), bf16),
            V((max(n_x - 1, 1), half, cpd, L), bf16),
            V((n_dp, cpd, L), bf16),
            V((n_dp - 1, cpd, L), bf16),
            V(sm, f32), V(sm, f32), V((n_x,) + sm, f32), V(sm, f32), V((n_win,) + sm, f32),
            V(sm, f32), V((n_dp,) + sm, f32),
            pltpu.SemaphoreType.DMA((copies,)), pltpu.SemaphoreType.DMA((copies,)),
            pltpu.SemaphoreType.DMA((5,)),
        ],
        compiler_params=pltpu.CompilerParams(
            collective_id=0, has_side_effects=True, vmem_limit_bytes=60 * 1024 * 1024),
        name="layer",
    )(tokens, target, gain[None, :], w_qkv, w_proj, table, index, maskv)

    s = everyone ** (-0.5)
    out = out.reshape(cpd, 4, hc).transpose(1, 2, 0)
    tot_heads = lax.dynamic_slice_in_dim(tot[:heads, :TABLE], lax.axis_index("mp") * nh, nh, 0)
    gain_gradient = tot[heads:heads + C // 256].reshape(C) * s
    loss = 0.5 * jnp.sum(tot[heads + C // 256]) / everyone
    return ig, out[:3], out[3], tot_heads.T * s, gain_gradient, loss


def solution(mesh):
    sizes = (mesh.shape["dp"], mesh.shape["win"], mesh.shape["mp"])
    in_specs = (
        P(("dp", "win", "mp"), None),
        P(("dp", "win", "mp"), None),
        P(("dp", "win"), None),
        P(),
        P(),
        P(None, "mp"),
        P(None, "mp", None),
        P("mp", None),
    )
    out_specs = (
        P(("dp", "win", "mp"), None),
        P(None, "mp", ("dp", "win")),
        P("mp", ("dp", "win")),
        P(None, "mp"),
        P(),
        P(),
    )
    return jax.shard_map(
        functools.partial(per_device, sizes), mesh=mesh, in_specs=in_specs, out_specs=out_specs,
        check_vma=False,
    )
```

time: 154 us -> 101 us (0.66)
  Pallas kernels: 121 us -> 88.6 us
  local copies, waits for them, and re-layouts: 18.8 us -> 7.6 us
  matrix products: 4.84 us -> 0 us
  other arithmetic: 6.08 us -> 2 us
    pallas_call x3 -> x1, Pallas kernels: 121 us -> 88.6 us  [per_device(): pl.pallas_call(functools.partial(layer_kernel, n_mp, n_win, n_dp, everyon...]
    reshape x7 -> x1, local copies, waits for them, and re-layouts: 8.74 us -> 1.2 us  [per_device(): out = out.reshape(cpd, 4, hc).transpose(1, 2, 0)]
    dot_general x2 -> x0, matrix products: 4.84 us -> none  [the longest x1 2.85 us: per_device(): jnp.dot(full, onehot, precision=lax.Precision.HIGHEST)]
    pad x2 -> x0, local copies, waits for them, and re-layouts: 1.72 us -> none  [padded(): return jnp.pad(a, ((0, 0), (0, PAD - WIN_TOK), (0, 0))).reshape(R, C)]
where the time goes in v1:
time: 101 us
  Pallas kernels  88.6 us (88%)
  local copies, waits for them, and re-layouts  7.6 us (8%)
  between operations  2.47 us (2%)
  other arithmetic  2 us (2%)
    pallas_call x1, Pallas kernels, per_device(): pl.pallas_call(functools.partial(layer_kernel, n_mp, n_win, n_dp, everyon...  88.6 us

profile of v1, /device:TPU:0, one launch (start us, length us, event | category | flops | bytes accessed | tf_op | source)
XLA Modules:
  0.0 100.7 jit_solution(4332022582380788699)
XLA Ops:
  0.6 0.0 copy-start
  0.6 0.0 copy-start.3
  0.7 1.3 %broadcast_in_dim.13.gain_ref = f32[1,768]{1,0:T(1,128)} reshape(f32[768]{0:T(1024)} %param.12) | data formatting | bytes 6144 | tf_op jit(solution)/shard_map/broadcast_in_dim | solution.py:499
  1.9 0.0 copy-done.3
  1.9 0.6 pad.12.table
  2.5 0.8 copy.14
  3.4 0.6 pad.13.index_ref
  4.0 0.0 copy-done
  4.0 0.8 compare_select_fusion.mask_ref
  4.8 88.6 %layer.1 = (f32[294,768]{1,0:T(8,128)}, f32[96,768]{1,0:T(8,128)}, f32[32,256]{1,0:T(8,128)}) custom-call(bf16[294,768]{1,0:T(8,128)(2,1)} %x_ref.1, bf16[294,768]{1,0:T(8,128)(2,1)} %t_ref.1, f32[1,768]{1,0:T(1,128)} %broadcast_in_dim.13.gain_ref, bf16[3,192,768]{2,1,0:T(8,128)(2,1)} %wqkv.1, bf16[192,768]{1,0:T(8,128)(2,1)} %wproj.1, f32[8,256]{1,0:T(8,128)} %pad.12.table, ...), custom_call_target="tpu_custom_call" | custom-call | tf_op jit(solution)/shard_map/layer/pallas_call | solution.py:470
  93.5 0.0 copy-start.1
  93.5 1.2 %copy.16 = f32[96,768]{0,1:T(8,128)S(1)} copy(f32[96,768]{1,0:T(8,128)} %get-tuple-element.10) | data formatting | bytes 589824 | tf_op jit(solution)/shard_map/reshape | solution.py:502
  94.7 0.7 slice.20
  95.4 0.0 copy-start.2
  95.4 0.6 slice_bitcast_fusion
  96.1 0.1 copy-done.2
  96.2 0.6 multiply_bitcast_fusion
  96.8 0.6 mul.28
  97.4 0.6 slice_reduce_fusion
  98.7 0.0 copy-done.1
  98.7 0.9 copy.18
  (4 shorter events, 0.0 us)
Async XLA Ops:
  0.6 3.4 %copy-start = (s32[24,49]{1,0:T(8,128)S(1)}, s32[24,49]{1,0:T(8,128)}, u32[]{:S(2)}) copy-start(s32[24,49]{1,0:T(8,128)} %param.10) | copy-start | bytes 14116
  0.6 1.3 %copy-start.3 = (f32[169,6]{0,1:T(8,128)S(1)}, f32[169,6]{0,1:T(8,128)}, u32[]{:S(2)}) copy-start(f32[169,6]{0,1:T(8,128)} %param.13) | copy-start | bytes 12172
  93.5 5.2 %copy-start.1 = (f32[294,768]{1,0:T(8,128)S(1)}, f32[294,768]{1,0:T(8,128)}, u32[]{:S(2)}) copy-start(f32[294,768]{1,0:T(8,128)} %get-tuple-element.18) | copy-start | bytes 2709508
  95.4 0.8 copy-start.2

commit v2 on v1

--- a/solution.py
+++ b/solution.py
@@ -274,7 +274,7 @@
             dq[r, c] = (dot(db, spread(ks[r, c]), 0, 0) * scale).astype(bf16)
         ds_ref[g] = total
 
-    waves = 2 if cpd % 32 == 0 else 1
+    waves = cpd // 32 if cpd % 32 == 0 else 1
     deep = cpd // waves
     xnt = xn[...].T
     gbt = gb[...].T
@@ -354,7 +354,7 @@
         y = add(a2[dp, rows(f)], *[rz[d, rows(f)] for d in range(n_dp - 1)])
         out_ref[rows(f), :] = y * everyone ** (-0.5)
 
-    for f in range(waves):
+    for f in range(min(waves, 2)):
         step1(f)
 
     @pl.loop(0, C // BN)
@@ -365,6 +365,9 @@
         y += dot(dv[...], w_ref[2, :, c], 1, 0)
         dxn[:, c] = y
 
+    step2(0)
+    for f in range(2, waves):
+        step1(f)
     gg[...] = jnp.zeros_like(gg)
 
     def finish(w):
@@ -380,7 +383,8 @@
     for w in range(W):
         finish(w)
 
-    step2(0)
+    if waves > 1:
+        step2(1)
     heads = n_mp * nh
     small[...] = jnp.zeros_like(small)
     hp = ng * PACK
@@ -401,7 +405,8 @@
     small[heads + C // BN:heads + C // BN + 1, :] = sq[...]
 
     cc0 = start(small, s_core, partner)
-    for f in range(1, waves):
+    step3(0)
+    for f in range(2, waves):
         step2(f)
 
     def share_small(src, slots, on, n):
@@ -421,13 +426,14 @@
     cc0.wait_recv()
     s1[...] = small[...] + s_core[...]
     cx = share_small(s1, sx, on_x, n_x)(x)
-    step3(0)
+    if waves > 1:
+        step3(1)
     finish_small(cx, s1, sx, x, n_x, s2)
     cw = share_small(s2, sw, on_win, n_win)(win)
+    for f in range(2, waves):
+        step3(f)
     finish_small(cw, s2, sw, win, n_win, s3)
     cz = share_small(s3, sz, on_dp, n_dp)(dp)
-    for f in range(1, waves):
-        step3(f)
     finish_small(cz, s3, sz, dp, n_dp, tot_ref)
     for f in range(waves):
         step4(f)
@@ -458,7 +464,7 @@
     cpd = C // (n_dp * n_win)
     L = 4 * hc
     half = n_dp // 2
-    waves = 2 if cpd % 32 == 0 else 1
+    waves = cpd // 32 if cpd % 32 == 0 else 1
     share = sharing(hc, n_win)
     copies = n_x + 4 * (n_x - 1) + 4 + (n_x - 1) * (1 + 4 * (2 * (share - 1) + 1))
     copies += waves * (n_x + 2 * (n_x - 1) + 2 * (n_win - 1) + n_dp - 1)

time: 101 us -> 98.3 us (0.973)
  Pallas kernels: 88.6 us -> 85.9 us
    pallas_call x1, Pallas kernels: 88.6 us -> 85.9 us  [per_device(): pl.pallas_call(functools.partial(layer_kernel, n_mp, n_win, n_dp, everyon...]
where the time goes in v2:
time: 98.3 us; the launch traced here: 97.9 us
  Pallas kernels  85.9 us (87%)
  local copies, waits for them, and re-layouts  7.6 us (8%)
  between operations  2.47 us (3%)
  other arithmetic  2 us (2%)
    pallas_call x1, Pallas kernels, per_device(): pl.pallas_call(functools.partial(layer_kernel, n_mp, n_win, n_dp, everyon...  85.9 us

profile of v2, /device:TPU:0, one launch (start us, length us, event | category | flops | bytes accessed | tf_op | source)
XLA Modules:
  0.0 97.9 jit_solution(4649503274461951635)
XLA Ops:
  0.6 0.0 copy-start
  0.6 0.0 copy-start.3
  0.7 1.3 %broadcast_in_dim.13.gain_ref = f32[1,768]{1,0:T(1,128)} reshape(f32[768]{0:T(1024)} %param.12) | data formatting | bytes 6144 | tf_op jit(solution)/shard_map/broadcast_in_dim | solution.py:505
  1.9 0.0 copy-done.3
  1.9 0.6 pad.12.table
  2.5 0.8 copy.14
  3.4 0.6 pad.13.index_ref
  4.0 0.0 copy-done
  4.0 0.8 compare_select_fusion.mask_ref
  4.8 85.9 %layer.1 = (f32[294,768]{1,0:T(8,128)}, f32[96,768]{1,0:T(8,128)}, f32[32,256]{1,0:T(8,128)}) custom-call(bf16[294,768]{1,0:T(8,128)(2,1)} %x_ref.1, bf16[294,768]{1,0:T(8,128)(2,1)} %t_ref.1, f32[1,768]{1,0:T(1,128)} %broadcast_in_dim.13.gain_ref, bf16[3,192,768]{2,1,0:T(8,128)(2,1)} %wqkv.1, bf16[192,768]{1,0:T(8,128)(2,1)} %wproj.1, f32[8,256]{1,0:T(8,128)} %pad.12.table, ...), custom_call_target="tpu_custom_call" | custom-call | tf_op jit(solution)/shard_map/layer/pallas_call | solution.py:476
  90.7 0.0 copy-start.1
  90.7 1.2 %copy.16 = f32[96,768]{0,1:T(8,128)S(1)} copy(f32[96,768]{1,0:T(8,128)} %get-tuple-element.10) | data formatting | bytes 589824 | tf_op jit(solution)/shard_map/reshape | solution.py:508
  91.9 0.7 slice.20
  92.7 0.0 copy-start.2
  92.7 0.6 slice_bitcast_fusion
  93.3 0.1 copy-done.2
  93.4 0.6 multiply_bitcast_fusion
  94.0 0.6 mul.28
  94.6 0.6 slice_reduce_fusion
  95.9 0.0 copy-done.1
  95.9 0.9 copy.18
  (4 shorter events, 0.0 us)
Async XLA Ops:
  0.6 3.4 %copy-start = (s32[24,49]{1,0:T(8,128)S(1)}, s32[24,49]{1,0:T(8,128)}, u32[]{:S(2)}) copy-start(s32[24,49]{1,0:T(8,128)} %param.10) | copy-start | bytes 14116
  0.6 1.3 %copy-start.3 = (f32[169,6]{0,1:T(8,128)S(1)}, f32[169,6]{0,1:T(8,128)}, u32[]{:S(2)}) copy-start(f32[169,6]{0,1:T(8,128)} %param.13) | copy-start | bytes 12172
  90.7 5.2 %copy-start.1 = (f32[294,768]{1,0:T(8,128)S(1)}, f32[294,768]{1,0:T(8,128)}, u32[]{:S(2)}) copy-start(f32[294,768]{1,0:T(8,128)} %get-tuple-element.18) | copy-start | bytes 2709508
  92.7 0.8 copy-start.2
